TPU v7x, 32 devices: a whole 2x2x4 slice. The times are simulated.
32 devices in a mesh: seq: 8 (over z, x), tp: 4 (over y, core).
Axes of the slice: x: 2, y: 2, z: 4, core: 2. Of those that a mesh axis runs over, the one named last changes fastest.
Arguments:
- tokens: bfloat16 [1024, 6144], P('seq', 'tp'), may hold values from -6 to 6
- router_weight: bfloat16 [6144, 8], P('tp'), may hold values from -0.15625 to 0.15625
- expert_ids: int32 [1024, 2], P('seq'), may hold values from 0 to 7, all different within a row; in each aligned block of 128 rows (0 to 127, 128 to 255, ...) at most 56 rows name the same one
- gate_weight: bfloat16 [8, 6144, 8192], P('seq', None, 'tp'), may hold values from -0.078125 to 0.078125
- up_weight: bfloat16 [8, 6144, 8192], P('seq', None, 'tp'), may hold values from -0.078125 to 0.078125
- down_weight: bfloat16 [8, 8192, 6144], P('seq', 'tp'), may hold values from -0.0625 to 0.0625
Outputs:
- mixed: bfloat16 [1024, 6144], P('seq', 'tp')
Inputs may be any that keep to these rules, and one draw needn't show every extreme that they name: `expert_ids`: each row names 2 different experts. In each aligned block of 128 rows (the tokens of one sequence group) no expert is named more than 56 times, a bound that some block reaches.
All inputs are finite; a program needn't handle non-finite values.
Results may differ from a plain program's by a relative error of at most 0.014.
Values may be sent and summed in bfloat16 or wider, within the bound.
A program may use at most 128 MiB of HBM per device.

v0:
```python
import jax
import jax.numpy as jnp
from jax import lax
from jax.sharding import PartitionSpec as P

D = 6144
CAP = 56


def slot_numbers(expert_ids, experts):
    flat_ids = expert_ids.reshape(-1)
    onehot = (flat_ids[:, None] == jnp.arange(experts, dtype=jnp.int32)[None, :]).astype(jnp.int32)
    before = jnp.cumsum(onehot, axis=0) - onehot
    return (flat_ids, jnp.sum(before * onehot, axis=1))


def per_device(tokens, router_weight, expert_ids, gate_weight, up_weight, down_weight):
    seq_count = lax.axis_size("seq")
    experts = router_weight.shape[1]
    halves = seq_count // experts
    tok_rows, top_count = expert_ids.shape
    capacity = CAP
    width = D
    gate_slab = gate_weight[0]
    up_slab = up_weight[0]
    down_slab = down_weight[0]
    partial_logits = jnp.dot(tokens, router_weight, preferred_element_type=jnp.float32)
    logits = lax.psum(partial_logits, "tp")
    chosen = expert_ids[:, :, None] == jnp.arange(experts, dtype=jnp.int32)[None, None, :]
    picked = jnp.sum(jnp.where(chosen, logits[:, None, :], 0.0), axis=2)
    gates = jax.nn.sigmoid(picked - picked[:, ::-1])
    flat_ids, slots = slot_numbers(expert_ids, experts)
    row_index = jnp.arange(seq_count * capacity, dtype=jnp.int32)
    row_expert = row_index // capacity // halves
    row_slot = row_index % capacity
    matches = (row_expert[:, None] == flat_ids[None, :]) & (row_slot[:, None] == slots[None, :])
    select = jnp.any(matches.reshape(seq_count * capacity, tok_rows, top_count), axis=2).astype(
        jnp.bfloat16
    )
    full_tokens = lax.all_gather(tokens, "tp", axis=1, tiled=True)
    outgoing = jnp.dot(select, full_tokens, preferred_element_type=jnp.float32).astype(jnp.bfloat16)
    outgoing = outgoing.reshape(seq_count, capacity, width)
    received = lax.all_to_all(outgoing, "seq", split_axis=0, concat_axis=0, tiled=True)
    count = received.shape[1]
    slot_rows = received.reshape(-1, width)
    gate = jnp.dot(slot_rows, gate_slab, preferred_element_type=jnp.float32)
    up = jnp.dot(slot_rows, up_slab, preferred_element_type=jnp.float32)
    hidden = (jax.nn.silu(gate) * up).astype(jnp.bfloat16)
    partial_value = jnp.dot(hidden, down_slab, preferred_element_type=jnp.float32).reshape(
        seq_count, count, width
    )
    reduced = lax.psum_scatter(
        partial_value.astype(jnp.bfloat16), "tp", scatter_dimension=2, tiled=True
    ).astype(jnp.float32)
    returned = lax.all_to_all(
        reduced.astype(jnp.bfloat16), "seq", split_axis=0, concat_axis=0, tiled=True
    ).astype(reduced.dtype)
    columns = returned.shape[2]
    summed = jnp.sum(returned.reshape(experts, halves, capacity, columns), axis=1)
    summed = summed.reshape(experts * capacity, columns)
    gathered = summed[flat_ids * capacity + slots].reshape(tok_rows, top_count, columns)
    mixed = jnp.sum(gathered * gates[:, :, None], axis=1)
    return mixed.astype(jnp.bfloat16)


def solution(mesh):
    in_specs = (
        P("seq", "tp"),
        P("tp", None),
        P("seq", None),
        P("seq", None, "tp"),
        P("seq", None, "tp"),
        P("seq", "tp", None),
    )
    out_specs = P("seq", "tp")
    return jax.shard_map(
        per_device, mesh=mesh, in_specs=in_specs, out_specs=out_specs, check_vma=False
    )
```

profile of v0, /device:TPU:0, one launch (start us, length us, event | category | flops | bytes accessed | tf_op | source)
XLA Modules:
  0.0 316.7 jit_solution(15803682167642336754)
XLA Ops:
  6.5 0.7 all-gather.2.cloned.1.call-update
  7.3 0.8 copy.16
  8.1 0.1 eq.78
  8.2 0.1 eq.74
  8.4 0.6 reduce-window.6
  9.0 0.2 slice_reduce_fusion
  9.3 0.1 eq.82
  9.6 0.9 and_reduce_fusion
  10.5 20.8 %all-gather.2.cloned.1.call-done = bf16[128,6144]{1,0:T(8,128)(2,1)} async-done(((bf16[128,1536]{1,0:T(8,128)(2,1)}), bf16[128,6144]{1,0:T(8,128)(2,1)}) %all-gather.2.cloned.1.call-update) | async-done | bytes 1572880 | tf_op jit(solution)/shard_map/all_gather | solution.py:40
  31.3 3.0 convolution_convert_fusion
  34.3 126.9 %all_to_all.10 = bf16[8,56,6144]{2,1,0:T(8,128)(2,1)S(1)} all-to-all(bf16[8,56,6144]{2,1,0:T(8,128)(2,1)S(1)} %bitcast.37), channel_id=1, replica_groups=mesh['seq'=8,'tp'=4] {'seq'}, dimensions={0} | all-to-all | bytes 11010048 | tf_op jit(solution)/shard_map/all_to_all | solution.py:43
  161.2 15.1 %fusion.4 = f32[448,2048]{1,0:T(8,128)S(1)} fusion(bf16[448,6144]{1,0:T(8,128)(2,1)S(1)} %bitcast.38, bf16[1,6144,2048]{2,1,0:T(8,128)(2,1)} %param.9), kind=kOutput, calls=%fused_computation.5 | convolution fusion | flops 11274289152 | bytes 34340864 | tf_op jit(solution)/shard_map/dot_general | solution.py:46
  176.3 16.8 %multiply_convert_fusion = bf16[448,2048]{1,0:T(8,128)(2,1)S(1)} fusion(f32[448,2048]{1,0:T(8,128)S(1)} %fusion.4, bf16[448,6144]{1,0:T(8,128)(2,1)S(1)} %bitcast.39, bf16[1,6144,2048]{2,1,0:T(8,128)(2,1)} %param.10), kind=kOutput, calls=%fused_computation.9 | convolution fusion | flops 11279794176 | bytes 36175872 | tf_op jit(solution)/shard_map/dot_general | solution.py:47
  193.1 18.0 %fusion.6 = bf16[8,56,6144]{2,1,0:T(8,128)(2,1)} fusion(bf16[8,56,2048]{2,1,0:T(8,128)(2,1)S(1)} %bitcast.42, bf16[1,2048,6144]{2,1,0:T(8,128)(2,1)} %param.11), kind=kOutput, calls=%fused_computation.7 | convolution fusion | flops 11277041664 | bytes 32505856 | tf_op jit(solution)/shard_map/dot_general | solution.py:49
  211.1 51.1 %reduce-scatter.2.cloned.1.call-done = bf16[8,56,1536]{2,1,0:T(8,128)(2,1)} async-done(((bf16[8,56,6144]{2,1,0:T(8,128)(2,1)}), bf16[8,56,1536]{2,1,0:T(8,128)(2,1)}) %reduce-scatter.2.cloned.1.call-update) | async-done | bytes 1376272 | tf_op jit(solution)/shard_map/reduce_scatter | solution.py:52
  262.3 5.5 %all-to-all-start.1 = ((bf16[8,56,1536]{2,1,0:T(8,128)(2,1)}), bf16[8,56,1536]{2,1,0:T(8,128)(2,1)}, u32[]{:S(2)}, u32[]{:S(2)}) async-start(bf16[8,56,1536]{2,1,0:T(8,128)(2,1)} %reduce-scatter.2.cloned.1.call-done), calls=%async_computation.2 | async-start | bytes 2752512 | tf_op jit(solution)/shard_map/all_to_all | solution.py:55
  267.9 0.1 mul.39
  268.1 0.2 fusion.21
  268.3 6.1 %psum.7 = f32[128,8]{0,1:T(8,128)S(1)} all-reduce(f32[128,8]{0,1:T(8,128)S(1)} %fusion.21), channel_id=1, replica_groups=mesh['seq'=8,'tp'=4] {'tp'}, use_global_device_ids=true, to_apply=%region_5.6 | all-reduce | flops 1024 | bytes 8192 | tf_op jit(solution)/shard_map/psum | solution.py:28
  274.6 26.0 %all-to-all-done.1 = bf16[8,56,1536]{2,1,0:T(8,128)(2,1)} async-done(((bf16[8,56,1536]{2,1,0:T(8,128)(2,1)}), bf16[8,56,1536]{2,1,0:T(8,128)(2,1)}, u32[]{:S(2)}, u32[]{:S(2)}) %all-to-all-start.1) | async-done | bytes 1376288 | tf_op jit(solution)/shard_map/all_to_all | solution.py:55
  300.5 1.7 bitcast_convert_fusion
  302.2 2.3 gather_fusion
  304.5 2.2 reshape.117
  306.8 3.0 multiply_reduce_fusion
  (23 shorter events, 0.6 us)
Async XLA Ops:
  6.5 261.5 %copy-start = (bf16[1536,8]{0,1:T(8,128)(2,1)S(1)}, bf16[1536,8]{0,1:T(8,128)(2,1)}, u32[]{:S(2)}) copy-start(bf16[1536,8]{0,1:T(8,128)(2,1)} %param.7) | copy-start | bytes 73732
  6.5 24.8 %all-gather.2.cloned.1.call-start = ((), (), s32[]{:S(2)}) async-start(), calls=%async_computation.3 | async-start | bytes 1966080 | tf_op jit(solution)/shard_map/all_gather | solution.py:40
  7.3 255.0 %reduce-scatter.2.cloned.1.call-start = ((), (), s32[]{:S(2)}) async-start(), calls=%async_computation.4 | async-start | bytes 6881280 | tf_op jit(solution)/shard_map/reduce_scatter | solution.py:52
  211.1 56.7 %copy-start.2 = (s32[128,2]{0,1:T(2,128)S(1)}, s32[128,2]{0,1:T(2,128)}, u32[]{:S(2)}) copy-start(s32[128,2]{0,1:T(2,128)} %param.8) | copy-start | bytes 3076
  211.1 56.9 %copy-start.1 = (bf16[128,1536]{1,0:T(8,128)(2,1)S(1)}, bf16[128,1536]{1,0:T(8,128)(2,1)}, u32[]{:S(2)}) copy-start(bf16[128,1536]{1,0:T(8,128)(2,1)} %param.6) | copy-start | bytes 1179652
  262.3 38.3 %all-to-all-start.1 = ((bf16[8,56,1536]{2,1,0:T(8,128)(2,1)}), bf16[8,56,1536]{2,1,0:T(8,128)(2,1)}, u32[]{:S(2)}, u32[]{:S(2)}) async-start(bf16[8,56,1536]{2,1,0:T(8,128)(2,1)} %reduce-scatter.2.cloned.1.call-done), calls=%async_computation.2 | async-start | bytes 2752512 | tf_op jit(solution)/shard_map/all_to_all | solution.py:55
Sparse Core Ops, SparseCore 0:
  8.9 22.3 all-gather.1
  211.3 50.9 reduce-scatter.1
where the time goes:
time: 317 us
  blocking collectives  133 us (42%)
  waiting for transfers between devices  98.6 us (31%)
  matrix products  53.1 us (17%)
  between operations  13.5 us (4%)
  local copies, waits for them, and re-layouts  6.46 us (2%)
  other arithmetic  6.39 us (2%)
  starting transfers between devices  5.55 us (2%)
    all_to_all x1, blocking collectives, per_device(): lax.all_to_all(outgoing, 'seq', split_axis=0, concat_axis=0, tiled=True)  127 us
    reduce_scatter x1, waiting for transfers between devices, per_device(): lax.psum_scatter(partial_value.astype(jnp.bfloat16), 'tp', scatter_dimens...  51.1 us
    all_to_all x1, waiting for transfers between devices, per_device(): lax.all_to_all(reduced.astype(jnp.bfloat16), 'seq', split_axis=0, concat_...  26 us
    all_gather x1, waiting for transfers between devices, per_device(): full_tokens = lax.all_gather(tokens, 'tp', axis=1, tiled=True)  20.8 us
    dot_general x1, matrix products, per_device(): jnp.dot(hidden, down_slab, preferred_element_type=jnp.float32)  18 us
    dot_general x1, matrix products, per_device(): up = jnp.dot(slot_rows, up_slab, preferred_element_type=jnp.float32)  16.8 us
    dot_general x1, matrix products, per_device(): gate = jnp.dot(slot_rows, gate_slab, preferred_element_type=jnp.float32)  15.1 us
  transfers between devices with their start and end apart: 3, of which 3 were waited for; matrix products, arithmetic and copies ran while one was open for 1% of the time, Pallas kernels for 0%

commit v1 on v0

v1 whole, which is shorter than its diff:
```python
import functools

import jax
import jax.numpy as jnp
from jax import lax
from jax.experimental import pallas as pl
from jax.experimental.pallas import tpu as pltpu
from jax.sharding import PartitionSpec as P

CAP = 56
CORES = 2


def slot_numbers(expert_ids, experts):
    flat_ids = expert_ids.reshape(-1)
    onehot = (flat_ids[:, None] == jnp.arange(experts, dtype=jnp.int32)[None, :]).astype(jnp.int32)
    before = jnp.cumsum(onehot, axis=0) - onehot
    return (flat_ids, jnp.sum(before * onehot, axis=1))


def flip(index, mask):
    bit = 1
    while bit <= mask:
        if mask & bit:
            index = index + (1 - 2 * ((index // bit) % 2)) * bit
        bit *= 2
    return index


def interleaved(seq):
    far, near = list(range(seq // 2, seq)), list(range(1, seq // 2))
    order = []
    while far or near:
        order += far[:1] + near[:1]
        far, near = far[1:], near[1:]
    return order


def remote(src, dst, send, recv, seq, tp):
    return pltpu.make_async_remote_copy(
        src_ref=src,
        dst_ref=dst,
        send_sem=send,
        recv_sem=recv,
        device_id={"seq": seq, "tp": tp},
        device_id_type=pl.DeviceIdType.MESH,
    )


def greet(seq, tp, s, t):
    barrier = pltpu.get_barrier_semaphore()
    for off in range(1, seq):
        pl.semaphore_signal(
            barrier, inc=1, device_id={"seq": flip(s, off), "tp": t}, device_id_type=pl.DeviceIdType.MESH
        )
    for off in range(1, tp):
        pl.semaphore_signal(
            barrier, inc=1, device_id={"seq": s, "tp": (t + off) % tp}, device_id_type=pl.DeviceIdType.MESH
        )
    pl.semaphore_wait(barrier, seq - 1 + tp - 1)


def dispatch_kernel(
    seq, tp, x_ref, part_ref, out_ref, logits_ref,
    local_sem, a_send, a_recv, d_send, d_recv, y_send, y_recv, f_send, f_recv, l_send, l_recv,
):
    s, t = lax.axis_index("seq"), lax.axis_index("tp")
    y, c = t // CORES, t % CORES
    rows = tp // CORES
    mate = y * CORES + 1 - c
    width = x_ref.shape[2]

    def block(group, shard):
        return out_ref.at[group, :, pl.ds(pl.multiple_of(shard * width, 128), width)]

    own = pltpu.make_async_copy(x_ref.at[s], block(s, t), local_sem.at[0])
    own.start()
    own_logits = pltpu.make_async_copy(part_ref, logits_ref.at[t], local_sem.at[1])
    own_logits.start()
    greet(seq, tp, s, t)
    order = interleaved(seq)
    sent = []
    spread = {}
    for off in order:
        spread[off] = remote(
            x_ref.at[flip(s, off)], block(s, t), a_send.at[off], a_recv.at[off], flip(s, off), t
        )
        spread[off].start()
    logit_copies = []
    for off in range(1, tp):
        copy = remote(
            part_ref, logits_ref.at[t], l_send.at[off], l_recv.at[off], s, (t + off) % tp
        )
        copy.start()
        logit_copies.append(copy)

    across = {}

    def relay(off):
        group = flip(s, off)
        for step in range(1, rows):
            across[off, step].wait_recv()
            origin = ((y + rows - step) % rows) * CORES + c
            copy = remote(
                block(group, origin), block(group, origin), f_send.at[step, off], f_recv.at[step, off], s, mate
            )
            copy.start()
            sent.append(copy)

    blocks = [0] + order
    for place, off in enumerate(blocks):
        group = flip(s, off)
        if off == 0:
            own.wait()
        else:
            spread[off].wait_recv()
        for step in range(1, rows):
            across[off, step] = remote(
                block(group, t), block(group, t), y_send.at[step, off], y_recv.at[step, off],
                s, ((y + step) % rows) * CORES + c,
            )
            across[off, step].start()
        copy = remote(block(group, t), block(group, t), d_send.at[off], d_recv.at[off], s, mate)
        copy.start()
        sent.append(copy)
        if place >= 2:
            relay(blocks[place - 2])
    for off in blocks[-2:]:
        relay(off)
    own_logits.wait()
    for copy in logit_copies:
        copy.wait()
    for copy in sent:
        copy.wait()
    for copy in across.values():
        copy.wait_send()
    for copy in spread.values():
        copy.wait_send()


def combine_kernel(
    seq, tp, p_ref, out_ref, mate_buf, half, across_buf, total,
    local_sem, a_send, a_recv, d_send, d_recv, y_send, y_recv,
):
    s, t = lax.axis_index("seq"), lax.axis_index("tp")
    y, c = t // CORES, t % CORES
    rows = tp // CORES
    mate = y * CORES + 1 - c
    width = out_ref.shape[2]

    def columns(shard):
        return pl.ds(pl.multiple_of(shard * width, 128), width)

    greet(seq, tp, s, t)
    order = list(range(seq // 2, seq)) + list(range(1, seq // 2)) + [0]
    pair = {}
    for off in order:
        group = flip(s, off)
        for step in list(range(1, rows)) + [0]:
            row = (y + step) % rows
            pair[off, step] = remote(
                p_ref.at[group, :, columns(row * CORES + 1 - c)], mate_buf.at[step, group],
                d_send.at[step, off], d_recv.at[step, off], s, mate,
            )
            pair[off, step].start()

    across = {}
    returned = {}

    def exchange(off):
        group = flip(s, off)
        for step in range(rows):
            row = (y + step) % rows
            pair[off, step].wait_recv()
            mine = p_ref[group, :, columns(row * CORES + c)].astype(jnp.float32)
            half[step, group] = (mine + mate_buf[step, group].astype(jnp.float32)).astype(jnp.bfloat16)
        for step in range(1, rows):
            across[off, step] = remote(
                half.at[step, group], across_buf.at[step, group], y_send.at[step, off], y_recv.at[step, off],
                s, ((y + step) % rows) * CORES + c,
            )
            across[off, step].start()

    def finish(off):
        group = flip(s, off)
        value = half[0, group].astype(jnp.float32)
        for step in range(1, rows):
            across[off, step].wait_recv()
            value = value + across_buf[step, group].astype(jnp.float32)
        total[group] = value.astype(jnp.bfloat16)
        if off == 0:
            copy = pltpu.make_async_copy(total.at[group], out_ref.at[s], local_sem)
        else:
            copy = remote(total.at[group], out_ref.at[s], a_send.at[off], a_recv.at[off], group, t)
        copy.start()
        returned[off] = copy

    for off in order:
        exchange(off)
    for off in order:
        finish(off)
    for copy in returned.values():
        copy.wait()
    for copy in across.values():
        copy.wait_send()
    for copy in pair.values():
        copy.wait_send()


def vmem(count):
    return [pl.BlockSpec(memory_space=pltpu.VMEM)] * count


def dispatch(seq, tp, outgoing, partial_logits):
    _, capacity, width = outgoing.shape
    rows = tp // CORES
    dma = pltpu.SemaphoreType.DMA
    return pl.pallas_call(
        functools.partial(dispatch_kernel, seq, tp),
        out_shape=(
            jax.ShapeDtypeStruct((seq, capacity, tp * width), jnp.bfloat16),
            jax.ShapeDtypeStruct((tp,) + partial_logits.shape, jnp.float32),
        ),
        in_specs=vmem(2),
        out_specs=tuple(vmem(2)),
        scratch_shapes=[
            dma((2,)), dma((seq,)), dma((seq,)), dma((seq,)), dma((seq,)),
            dma((rows, seq)), dma((rows, seq)), dma((rows, seq)), dma((rows, seq)),
            dma((tp,)), dma((tp,)),
        ],
        compiler_params=pltpu.CompilerParams(collective_id=0, has_side_effects=True),
        name="dispatch",
    )(outgoing, partial_logits)


def combine(seq, tp, partial_value):
    _, capacity, full = partial_value.shape
    width = full // tp
    rows = tp // CORES
    dma = pltpu.SemaphoreType.DMA
    return pl.pallas_call(
        functools.partial(combine_kernel, seq, tp),
        out_shape=jax.ShapeDtypeStruct((seq, capacity, width), jnp.bfloat16),
        in_specs=vmem(1),
        out_specs=vmem(1)[0],
        scratch_shapes=[
            pltpu.VMEM((rows, seq, capacity, width), jnp.bfloat16),
            pltpu.VMEM((rows, seq, capacity, width), jnp.bfloat16),
            pltpu.VMEM((rows, seq, capacity, width), jnp.bfloat16),
            pltpu.VMEM((seq, capacity, width), jnp.bfloat16),
            dma, dma((seq,)), dma((seq,)), dma((rows, seq)), dma((rows, seq)),
            dma((rows, seq)), dma((rows, seq)),
        ],
        compiler_params=pltpu.CompilerParams(collective_id=1, has_side_effects=True),
        name="combine",
    )(partial_value)


def per_device(seq, tp, tokens, router_weight, expert_ids, gate_weight, up_weight, down_weight):
    experts = router_weight.shape[1]
    halves = seq // experts
    tok_rows, top_count = expert_ids.shape
    flat_ids, slots = slot_numbers(expert_ids, experts)
    row_index = jnp.arange(seq * CAP, dtype=jnp.int32)
    row_expert = row_index // CAP // halves
    row_slot = row_index % CAP
    matches = (row_expert[:, None] == flat_ids[None, :]) & (row_slot[:, None] == slots[None, :])
    matches = matches.reshape(seq * CAP, tok_rows, top_count)
    select = jnp.any(matches, axis=2).astype(jnp.bfloat16)
    partial_logits = lax.dot_general(
        router_weight, tokens, (((0,), (1,)), ((), ())), preferred_element_type=jnp.float32
    )
    outgoing = jnp.dot(select, tokens, preferred_element_type=jnp.float32).astype(jnp.bfloat16)
    received, logit_parts = dispatch(seq, tp, outgoing.reshape(seq, CAP, -1), partial_logits)
    slot_rows = received.reshape(seq * CAP, -1)
    gate = jnp.dot(slot_rows, gate_weight[0], preferred_element_type=jnp.float32)
    up = jnp.dot(slot_rows, up_weight[0], preferred_element_type=jnp.float32)
    hidden = (jax.nn.silu(gate) * up).astype(jnp.bfloat16)
    partial_value = jnp.dot(hidden, down_weight[0], preferred_element_type=jnp.float32)
    returned = combine(seq, tp, partial_value.astype(jnp.bfloat16).reshape(seq, CAP, -1))

    logits = jnp.sum(logit_parts, axis=0).T
    chosen = expert_ids[:, :, None] == jnp.arange(experts, dtype=jnp.int32)[None, None, :]
    picked = jnp.sum(jnp.where(chosen, logits[:, None, :], 0.0), axis=2)
    gates = jax.nn.sigmoid(picked - picked[:, ::-1])
    weights = jnp.sum(jnp.where(matches, gates[None, :, :], 0.0), axis=2).T
    high = lax.reduce_precision(weights, 8, 7)
    low = weights - high
    summed = returned.reshape(seq * CAP, -1)
    mixed = jnp.dot(high.astype(jnp.bfloat16), summed, preferred_element_type=jnp.float32)
    mixed = mixed + jnp.dot(low.astype(jnp.bfloat16), summed, preferred_element_type=jnp.float32)
    return mixed.astype(jnp.bfloat16)


def solution(mesh):
    in_specs = (
        P("seq", "tp"),
        P("tp", None),
        P("seq", None),
        P("seq", None, "tp"),
        P("seq", None, "tp"),
        P("seq", "tp", None),
    )
    step = functools.partial(per_device, mesh.shape["seq"], mesh.shape["tp"])
    return jax.shard_map(
        step, mesh=mesh, in_specs=in_specs, out_specs=P("seq", "tp"), check_vma=False
    )
```

time: 317 us -> 160 us (0.50)
  blocking collectives: 133 us -> 0 us
  waiting for transfers between devices: 98.6 us -> 0 us
  Pallas kernels: 0 us -> 97.6 us
  between operations: 13.5 us -> 0.14 us
  matrix products: 53.1 us -> 58.8 us
  starting transfers between devices: 5.55 us -> 0 us
  local copies, waits for them, and re-layouts: 6.46 us -> 1.58 us
  other arithmetic: 6.39 us -> 1.86 us
    all_to_all x1 -> x0, blocking collectives: 127 us -> none  [per_device(): lax.all_to_all(outgoing, 'seq', split_axis=0, concat_axis=0, tiled=True)]
    pallas_call x0 -> x2, Pallas kernels: none -> 97.6 us  [the longest x1 53 us: dispatch(): pl.pallas_call(functools.partial(dispatch_kernel, seq, tp), out_shape=(ja...]
    reduce_scatter x1 -> x0, waiting for transfers between devices: 51.1 us -> none  [per_device(): lax.psum_scatter(partial_value.astype(jnp.bfloat16), 'tp', scatter_dimens...]
    all_to_all x1 -> x0, waiting for transfers between devices: 26 us -> none  [per_device(): lax.all_to_all(reduced.astype(jnp.bfloat16), 'seq', split_axis=0, concat_...]
    all_gather x1 -> x0, waiting for transfers between devices: 20.8 us -> none  [per_device(): full_tokens = lax.all_gather(tokens, 'tp', axis=1, tiled=True)]
    psum x1 -> x0, blocking collectives: 6.1 us -> none  [per_device(): logits = lax.psum(partial_logits, 'tp')]
    dot_general x5 -> x7, matrix products: 53.1 us -> 58.8 us  [the longest x1 18 us: per_device(): jnp.dot(hidden, down_weight[0], preferred_element_type=jnp.float32)]
    all_to_all x1 -> x0, starting transfers between devices: 5.51 us -> none  [per_device(): lax.all_to_all(reduced.astype(jnp.bfloat16), 'seq', split_axis=0, concat_...]
  transfers between devices with their start and end apart: 3 -> 0, of which waited for: 3 -> 0; matrix products, arithmetic and copies ran while one was open for 1% -> 0% of each run, Pallas kernels for 0% -> 0%
where the time goes in v1:
time: 160 us
  Pallas kernels  97.6 us (61%)
  matrix products  58.8 us (37%)
  other arithmetic  1.86 us (1%)
    pallas_call x1, Pallas kernels, dispatch(): pl.pallas_call(functools.partial(dispatch_kernel, seq, tp), out_shape=(ja...  53 us
    pallas_call x1, Pallas kernels, combine(): pl.pallas_call(functools.partial(combine_kernel, seq, tp), out_shape=jax....  44.6 us
    dot_general x1, matrix products, per_device(): jnp.dot(hidden, down_weight[0], preferred_element_type=jnp.float32)  18 us
    dot_general x1, matrix products, per_device(): up = jnp.dot(slot_rows, up_weight[0], preferred_element_type=jnp.float32)  16.8 us
    dot_general x1, matrix products, per_device(): jnp.dot(slot_rows, gate_weight[0], preferred_element_type=jnp.float32)  16.6 us

profile of v1, /device:TPU:0, one launch (start us, length us, event | category | flops | bytes accessed | tf_op | source)
XLA Modules:
  0.0 159.9 jit_solution(16980247608319799808)
XLA Ops:
  0.0 0.0 copy-start
  0.0 0.8 copy.18
  0.8 0.1 eq.78
  1.0 0.6 reduce-window.6
  1.6 0.2 slice_reduce_fusion
  1.8 0.1 eq.74
  2.0 0.1 fusion.17
  2.1 0.1 eq.82
  2.2 0.1 copy.20
  2.3 0.9 fusion.12
  3.2 0.0 copy-done
  3.2 1.6 %convolution_convert_fusion = bf16[448,1536]{1,0:T(8,128)(2,1)} fusion(pred[448,128]{1,0:T(8,128)(4,1)S(1)} %fusion.12, bf16[128,1536]{1,0:T(8,128)(2,1)S(1)} %copy-done), kind=kOutput, calls=%fused_computation.8 | convolution fusion | flops 176848896 | bytes 1826816 | tf_op jit(solution)/shard_map/dot_general | solution.py:273
  4.9 1.5 fusion.26.part_ref
  6.4 53.0 %dispatch.1 = (bf16[8,56,6144]{2,1,0:T(8,128)(2,1)}, f32[4,8,128]{2,1,0:T(8,128)}) custom-call(bf16[8,56,1536]{2,1,0:T(8,128)(2,1)} %bitcast.42, f32[8,128]{1,0:T(8,128)} %fusion.26.part_ref), custom_call_target="tpu_custom_call" | custom-call | tf_op jit(solution)/shard_map/dispatch/pallas_call | solution.py:218
  59.4 0.0 copy-start.4
  59.4 16.6 %fusion.4 = f32[448,2048]{1,0:T(8,128)S(1)} fusion(bf16[448,6144]{1,0:T(8,128)(2,1)} %bitcast.45, bf16[1,6144,2048]{2,1,0:T(8,128)(2,1)} %param.9), kind=kOutput, calls=%fused_computation.4 | convolution fusion | flops 11274289152 | bytes 34340864 | tf_op jit(solution)/shard_map/dot_general | solution.py:276
  76.0 0.0 copy-done.4
  76.1 16.8 %multiply_convert_fusion = bf16[448,2048]{1,0:T(8,128)(2,1)S(1)} fusion(f32[448,2048]{1,0:T(8,128)S(1)} %fusion.4, bf16[448,6144]{1,0:T(8,128)(2,1)S(1)} %bitcast.46, bf16[1,6144,2048]{2,1,0:T(8,128)(2,1)} %param.10), kind=kOutput, calls=%fused_computation.7 | convolution fusion | flops 11279794176 | bytes 36175872 | tf_op jit(solution)/shard_map/dot_general | solution.py:277
  92.9 18.0 %fusion.6 = bf16[448,6144]{1,0:T(8,128)(2,1)} fusion(bf16[448,2048]{1,0:T(8,128)(2,1)S(1)} %multiply_convert_fusion, bf16[1,2048,6144]{2,1,0:T(8,128)(2,1)} %param.11), kind=kOutput, calls=%fused_computation.6 | convolution fusion | flops 11277041664 | bytes 32505856 | tf_op jit(solution)/shard_map/dot_general | solution.py:279
  110.8 44.6 %combine.1 = bf16[8,56,1536]{2,1,0:T(8,128)(2,1)} custom-call(bf16[8,56,6144]{2,1,0:T(8,128)(2,1)} %bitcast.43), custom_call_target="tpu_custom_call" | custom-call | tf_op jit(solution)/shard_map/combine/pallas_call | solution.py:241
  155.4 0.0 copy-done.2
  155.5 0.2 select_reduce_fusion
  155.7 1.7 %fusion.15 = f32[128,1536]{1,0:T(8,128)S(1)} fusion(bf16[448,1536]{1,0:T(8,128)(2,1)} %bitcast.40, f32[448,128]{1,0:T(8,128)S(1)} %select_reduce_fusion), kind=kOutput, calls=%fused_computation.17 | convolution fusion | flops 176275456 | bytes 2392064 | tf_op jit(solution)/shard_map/dot_general | solution.py:290
  157.5 2.5 %fusion.11 = bf16[128,1536]{1,0:T(8,128)(2,1)} fusion(f32[128,1536]{1,0:T(8,128)S(1)} %fusion.15, bf16[448,1536]{1,0:T(8,128)(2,1)} %bitcast.41, f32[448,128]{1,0:T(8,128)S(1)} %select_reduce_fusion), kind=kOutput, calls=%fused_computation.10 | convolution fusion | flops 176726016 | bytes 2785280 | tf_op jit(solution)/shard_map/dot_general | solution.py:291
  (13 shorter events, 0.2 us)
Async XLA Ops:
  0.0 3.2 %copy-start = (bf16[128,1536]{1,0:T(8,128)(2,1)S(1)}, bf16[128,1536]{1,0:T(8,128)(2,1)}, u32[]{:S(2)}) copy-start(bf16[128,1536]{1,0:T(8,128)(2,1)} %param.6) | copy-start | bytes 1179652
  59.4 16.6 %copy-start.4 = (bf16[8,56,6144]{2,1,0:T(8,128)(2,1)S(1)}, bf16[8,56,6144]{2,1,0:T(8,128)(2,1)}, u32[]{:S(2)}) copy-start(bf16[8,56,6144]{2,1,0:T(8,128)(2,1)} %get-tuple-element.8) | copy-start | bytes 16515076
  110.8 44.6 %copy-start.2 = (f32[4,8,128]{2,1,0:T(8,128)S(1)}, f32[4,8,128]{2,1,0:T(8,128)}, u32[]{:S(2)}) copy-start(f32[4,8,128]{2,1,0:T(8,128)} %get-tuple-element.7) | copy-start | bytes 49156
  110.8 44.6 %copy-start.3 = (s32[128,2]{0,1:T(2,128)S(1)}, s32[128,2]{0,1:T(2,128)}, u32[]{:S(2)}) copy-start(s32[128,2]{0,1:T(2,128)} %param.8) | copy-start | bytes 3076
  110.8 49.1 %copy-start.1 = (bf16[128,1536]{1,0:T(8,128)(2,1)S(1)}, bf16[128,1536]{1,0:T(8,128)(2,1)}, u32[]{:S(2)}) copy-start(bf16[128,1536]{1,0:T(8,128)(2,1)} %param.6) | copy-start | bytes 1179652
